TPU v7x, 128 devices: a whole 4x4x4 slice. The times are simulated.
128 devices in a mesh: ctx: 16 (over z_lo, y, core), head: 8 (over x, z_hi).
Axes of the slice: x: 4, y: 4, z: 4 (z_hi: 2, z_lo: 2; z = z_hi * 2 + z_lo), core: 2. Of those that a mesh axis runs over, the one named last changes fastest.
Arguments:
- queries: bfloat16 [16384, 6144], P(('ctx', 'head')), may hold values from -56 to 56
- key_rows: bfloat16 [16384, 6144], P(('ctx', 'head')), may hold values from -6 to 6
- value_rows: bfloat16 [16384, 6144], P(('ctx', 'head')), may hold values from -6 to 6
- key_tiles: int32 [48, 128, 18], P('head', 'ctx'), may hold values from -1 to 127, as said below
Outputs:
- attended: bfloat16 [16384, 6144], P(('ctx', 'head'))
Inputs may be any that keep to these rules, and one draw needn't show every extreme that they name: In key_tiles[h, i] the live slots come first and name distinct tiles whose time slab differs from tile i's by at most one; the rest hold -1. Tile i itself and the tiles of the same cell one time slab before and after (where they exist) are always live. In every draw some head and tile have all 18 slots live.
All inputs are finite; a program needn't handle non-finite values.
Results may differ from a plain program's by a relative error of at most 0.0046.
Values may be sent and summed in bfloat16 or wider, within the bound.
A program may use at most 128 MiB of HBM per device.

v0:
```python
import jax
import jax.numpy as jnp
from jax import lax
from jax.sharding import PartitionSpec as P

HDIM = 128
TILE = 128
GY = 2
GX = 4
TT_DEV = 1


masked_score = -1e30


def padded_2(block, sides, width):
    for axis, dim in sides:
        count = lax.axis_size(axis)
        forward = [(i, i + 1) for i in range(count - 1)]
        backward = [(target, source) for source, target in forward]
        low = lax.ppermute(
            lax.slice_in_dim(block, block.shape[dim] - width, None, axis=dim), axis, forward
        )
        high = lax.ppermute(lax.slice_in_dim(block, 0, width, axis=dim), axis, backward)
        block = jnp.concatenate([low, block, high], axis=dim)
    return block


def attend_all(head_query, head_pairs, is_live, local_ids):
    chosen_keys = head_pairs[0][local_ids]
    chosen_values = head_pairs[1][local_ids]
    scores = jnp.einsum(
        "qtd,qksd->qtks", head_query, chosen_keys, preferred_element_type=jnp.float32
    ) * HDIM ** (-0.5)
    live_mask = is_live[:, None, :, None]
    scores = jnp.where(live_mask, scores, masked_score)
    row_max = jnp.max(scores, axis=(2, 3), keepdims=True)
    weight = jnp.where(live_mask, jnp.exp(scores - row_max), 0.0)
    row_total = jnp.sum(weight, axis=(2, 3))
    probs = weight.astype(jnp.bfloat16)
    numerator = jnp.einsum(
        "qtks,qksd->qtd", probs, chosen_values, preferred_element_type=jnp.float32
    )
    return (numerator / row_total[..., None]).astype(jnp.bfloat16)


def shards(queries, key_rows, value_rows, key_tiles):
    cells = GY * GX
    context = lax.axis_index("ctx")
    moved_query, moved_keys, moved_values = (
        lax.all_to_all(queries, "head", split_axis=1, concat_axis=0, tiled=True),
        lax.all_to_all(key_rows, "head", split_axis=1, concat_axis=0, tiled=True),
        lax.all_to_all(value_rows, "head", split_axis=1, concat_axis=0, tiled=True),
    )
    columns = moved_query.shape[1]
    stacked_pairs = jnp.stack((moved_keys, moved_values))
    local_query = moved_query.reshape(TT_DEV * cells, TILE, columns)
    tile_base = (context * TT_DEV - 1) * cells
    padded = padded_2(stacked_pairs, (("ctx", 1),), cells * TILE)
    extended = padded.reshape(2, (TT_DEV + 2) * cells, TILE, columns)
    heads_dev = key_tiles.shape[0]

    def one_head(head_index):
        head_query = lax.dynamic_slice_in_dim(local_query, head_index * HDIM, HDIM, 2)
        head_pairs = lax.dynamic_slice_in_dim(extended, head_index * HDIM, HDIM, 3)
        listed = lax.dynamic_index_in_dim(key_tiles, head_index, 0, keepdims=False)
        is_live = listed >= 0
        local_ids = jnp.where(is_live, listed - tile_base, 0)
        return attend_all(head_query, head_pairs, is_live, local_ids)

    result = lax.map(one_head, jnp.arange(heads_dev, dtype=jnp.int32))
    block_rows = result.shape[1] * result.shape[2]
    regrouped = result.transpose(1, 2, 0, 3).reshape(block_rows, heads_dev * HDIM)
    return lax.all_to_all(regrouped, "head", split_axis=0, concat_axis=1, tiled=True)


def solution(mesh):
    placed = (
        P(("ctx", "head"), None),
        P(("ctx", "head"), None),
        P(("ctx", "head"), None),
        P("head", "ctx", None),
    )
    return jax.shard_map(
        shards, mesh=mesh, in_specs=placed, out_specs=P(("ctx", "head"), None), check_vma=False
    )
```

profile of v0, /device:TPU:6, one launch (start us, length us, event | category | flops | bytes accessed | tf_op | source)
XLA Modules:
  0.0 364.4 jit_solution(16916242534798642506)
XLA Ops:
  3.5 8.1 %all-to-all-start.1 = ((bf16[128,8,768]{2,0,1:T(8,128)(2,1)}), bf16[128,8,768]{2,0,1:T(8,128)(2,1)S(1)}, u32[]{:S(2)}, u32[]{:S(2)}) async-start(bf16[128,8,768]{2,0,1:T(8,128)(2,1)} %copy.23), calls=%async_computation.1 | async-start | bytes 3145728 | tf_op jit(solution)/shard_map/all_to_all | solution.py:52
  15.1 16.7 %all-to-all-done.1 = bf16[128,8,768]{2,0,1:T(8,128)(2,1)S(1)} async-done(((bf16[128,8,768]{2,0,1:T(8,128)(2,1)}), bf16[128,8,768]{2,0,1:T(8,128)(2,1)S(1)}, u32[]{:S(2)}, u32[]{:S(2)}) %all-to-all-start.1) | async-done | bytes 1572896 | tf_op jit(solution)/shard_map/all_to_all | solution.py:52
  31.7 26.8 %all_to_all.67 = bf16[128,8,768]{2,0,1:T(8,128)(2,1)S(1)} all-to-all(bf16[128,8,768]{2,0,1:T(8,128)(2,1)} %copy.25), channel_id=1, replica_groups=mesh['ctx'=16,'head'=8] {'head'}, dimensions={1} | all-to-all | bytes 3145728 | tf_op jit(solution)/shard_map/all_to_all | solution.py:53
  67.3 6.4 %all-to-all-start = ((bf16[128,8,768]{0,2,1:T(8,128)(2,1)}), bf16[128,8,768]{0,2,1:T(8,128)(2,1)}, u32[]{:S(2)}, u32[]{:S(2)}) async-start(bf16[128,8,768]{0,2,1:T(8,128)(2,1)} %bitcast.79), calls=%async_computation | async-start | bytes 3145728 | tf_op jit(solution)/shard_map/all_to_all | solution.py:51
  73.7 7.8 %pad_maximum_fusion = bf16[2,3072,768]{2,1,0:T(8,128)(2,1)} fusion(bf16[2,1024,768]{2,1,0:T(8,128)(2,1)} %collective-permute-done.1, bf16[1,1024,768]{2,1,0:T(8,128)(2,1)S(1)} %bitcast.78, bf16[1,1024,768]{2,1,0:T(8,128)(2,1)S(1)} %bitcast.76, bf16[2,1024,768]{2,1,0:T(8,128)(2,1)} %collective-permute-done), kind=kLoop, calls=%fused_computation.26 | loop fusion | flops 37748736 | bytes 18874368 | tf_op jit(solution)/shard_map/concatenate | solution.py:25
  81.5 37.7 %all-to-all-done = bf16[128,8,768]{0,2,1:T(8,128)(2,1)} async-done(((bf16[128,8,768]{0,2,1:T(8,128)(2,1)}), bf16[128,8,768]{0,2,1:T(8,128)(2,1)}, u32[]{:S(2)}, u32[]{:S(2)}) %all-to-all-start) | async-done | bytes 1572896 | tf_op jit(solution)/shard_map/all_to_all | solution.py:51
  119.2 217.1 %while.10 = (s32[]{:T(128)}, bf16[6,8,128,128]{2,3,0,1:T(8,128)(2,1)}, s32[6]{0:T(128)S(1)}, s32[6,8,18]{2,1,0:T(8,128)}, bf16[8,128,768]{1,2,0:T(8,128)(2,1)}, ...) while((s32[]{:T(128)}, ...), condition=%wide.region_3.4_spmd, body=%wide.region_0.3_spmd.sunk | while | flops 1238892416 | bytes 99120400 | solution.py:71
  124.3 7.6 %gather_fusion.1 = bf16[144,128,128]{2,1,0:T(8,128)(2,1)} fusion(bf16[24,128,128]{2,1,0:T(8,128)(2,1)S(1)} %get-tuple-element.136, s32[1024]{0:T(1024)S(1)} %pad_clamp_fusion.2), kind=kCustom, calls=%fused_computation.clone.1 | custom fusion | bytes 9437760 | tf_op jit(solution)/shard_map/while/body/eval_jaxpr/gather | solution.py:30
  131.9 3.4 fusion.36
  139.0 7.5 %gather_fusion = bf16[144,128,128]{2,1,0:T(8,128)(2,1)} fusion(bf16[24,128,128]{2,1,0:T(8,128)(2,1)S(1)} %get-tuple-element.133, s32[1024]{0:T(1024)S(1)} %pad_clamp_fusion.2), kind=kCustom, calls=%fused_computation.1.clone.1 | custom fusion | bytes 9437760 | tf_op jit(solution)/shard_map/while/body/eval_jaxpr/gather | solution.py:31
  146.5 7.9 %fusion.38 = bf16[1,8,128,128]{3,2,1,0:T(8,128)(2,1)S(1)} fusion(bf16[8,18,128,128]{3,2,1,0:T(8,128)(2,1)} %bitcast.73, f32[8,128,18,128]{1,3,2,0:T(8,128)} %copy-done, f32[8,128]{1,0:T(8,128)S(1)} %get-tuple-element.138, pred[8,18]{1,0:T(8,128)(4,1)S(1)} %bitcast.86, f32[8,128]{1,0:T(8,128)S(1)} %fusion.37), kind=kOutput, calls=%fused_computation.12.clone.1 | convolution fusion | flops 616038400 | bytes 14426256 | tf_op jit(solution)/shard_map/while/body/eval_jaxpr/qtks,qksd->qtd/dot_general | solution.py:41
  160.5 7.6 %gather_fusion.1 = bf16[144,128,128]{2,1,0:T(8,128)(2,1)} fusion(bf16[24,128,128]{2,1,0:T(8,128)(2,1)S(1)} %get-tuple-element.136, s32[1024]{0:T(1024)S(1)} %pad_clamp_fusion.2), kind=kCustom, calls=%fused_computation.clone.1 | custom fusion | bytes 9437760 | tf_op jit(solution)/shard_map/while/body/eval_jaxpr/gather | solution.py:30
  168.1 3.4 fusion.36
  175.2 7.5 %gather_fusion = bf16[144,128,128]{2,1,0:T(8,128)(2,1)} fusion(bf16[24,128,128]{2,1,0:T(8,128)(2,1)S(1)} %get-tuple-element.133, s32[1024]{0:T(1024)S(1)} %pad_clamp_fusion.2), kind=kCustom, calls=%fused_computation.1.clone.1 | custom fusion | bytes 9437760 | tf_op jit(solution)/shard_map/while/body/eval_jaxpr/gather | solution.py:31
  182.7 7.9 %fusion.38 = bf16[1,8,128,128]{3,2,1,0:T(8,128)(2,1)S(1)} fusion(bf16[8,18,128,128]{3,2,1,0:T(8,128)(2,1)} %bitcast.73, f32[8,128,18,128]{1,3,2,0:T(8,128)} %copy-done, f32[8,128]{1,0:T(8,128)S(1)} %get-tuple-element.138, pred[8,18]{1,0:T(8,128)(4,1)S(1)} %bitcast.86, f32[8,128]{1,0:T(8,128)S(1)} %fusion.37), kind=kOutput, calls=%fused_computation.12.clone.1 | convolution fusion | flops 616038400 | bytes 14426256 | tf_op jit(solution)/shard_map/while/body/eval_jaxpr/qtks,qksd->qtd/dot_general | solution.py:41
  196.7 7.6 %gather_fusion.1 = bf16[144,128,128]{2,1,0:T(8,128)(2,1)} fusion(bf16[24,128,128]{2,1,0:T(8,128)(2,1)S(1)} %get-tuple-element.136, s32[1024]{0:T(1024)S(1)} %pad_clamp_fusion.2), kind=kCustom, calls=%fused_computation.clone.1 | custom fusion | bytes 9437760 | tf_op jit(solution)/shard_map/while/body/eval_jaxpr/gather | solution.py:30
  204.3 3.4 fusion.36
  211.4 7.5 %gather_fusion = bf16[144,128,128]{2,1,0:T(8,128)(2,1)} fusion(bf16[24,128,128]{2,1,0:T(8,128)(2,1)S(1)} %get-tuple-element.133, s32[1024]{0:T(1024)S(1)} %pad_clamp_fusion.2), kind=kCustom, calls=%fused_computation.1.clone.1 | custom fusion | bytes 9437760 | tf_op jit(solution)/shard_map/while/body/eval_jaxpr/gather | solution.py:31
  218.9 7.9 %fusion.38 = bf16[1,8,128,128]{3,2,1,0:T(8,128)(2,1)S(1)} fusion(bf16[8,18,128,128]{3,2,1,0:T(8,128)(2,1)} %bitcast.73, f32[8,128,18,128]{1,3,2,0:T(8,128)} %copy-done, f32[8,128]{1,0:T(8,128)S(1)} %get-tuple-element.138, pred[8,18]{1,0:T(8,128)(4,1)S(1)} %bitcast.86, f32[8,128]{1,0:T(8,128)S(1)} %fusion.37), kind=kOutput, calls=%fused_computation.12.clone.1 | convolution fusion | flops 616038400 | bytes 14426256 | tf_op jit(solution)/shard_map/while/body/eval_jaxpr/qtks,qksd->qtd/dot_general | solution.py:41
  232.9 7.6 %gather_fusion.1 = bf16[144,128,128]{2,1,0:T(8,128)(2,1)} fusion(bf16[24,128,128]{2,1,0:T(8,128)(2,1)S(1)} %get-tuple-element.136, s32[1024]{0:T(1024)S(1)} %pad_clamp_fusion.2), kind=kCustom, calls=%fused_computation.clone.1 | custom fusion | bytes 9437760 | tf_op jit(solution)/shard_map/while/body/eval_jaxpr/gather | solution.py:30
  240.5 3.4 fusion.36
  247.5 7.5 %gather_fusion = bf16[144,128,128]{2,1,0:T(8,128)(2,1)} fusion(bf16[24,128,128]{2,1,0:T(8,128)(2,1)S(1)} %get-tuple-element.133, s32[1024]{0:T(1024)S(1)} %pad_clamp_fusion.2), kind=kCustom, calls=%fused_computation.1.clone.1 | custom fusion | bytes 9437760 | tf_op jit(solution)/shard_map/while/body/eval_jaxpr/gather | solution.py:31
  255.1 7.9 %fusion.38 = bf16[1,8,128,128]{3,2,1,0:T(8,128)(2,1)S(1)} fusion(bf16[8,18,128,128]{3,2,1,0:T(8,128)(2,1)} %bitcast.73, f32[8,128,18,128]{1,3,2,0:T(8,128)} %copy-done, f32[8,128]{1,0:T(8,128)S(1)} %get-tuple-element.138, pred[8,18]{1,0:T(8,128)(4,1)S(1)} %bitcast.86, f32[8,128]{1,0:T(8,128)S(1)} %fusion.37), kind=kOutput, calls=%fused_computation.12.clone.1 | convolution fusion | flops 616038400 | bytes 14426256 | tf_op jit(solution)/shard_map/while/body/eval_jaxpr/qtks,qksd->qtd/dot_general | solution.py:41
  269.1 7.6 %gather_fusion.1 = bf16[144,128,128]{2,1,0:T(8,128)(2,1)} fusion(bf16[24,128,128]{2,1,0:T(8,128)(2,1)S(1)} %get-tuple-element.136, s32[1024]{0:T(1024)S(1)} %pad_clamp_fusion.2), kind=kCustom, calls=%fused_computation.clone.1 | custom fusion | bytes 9437760 | tf_op jit(solution)/shard_map/while/body/eval_jaxpr/gather | solution.py:30
  276.7 3.4 fusion.36
  283.7 7.5 %gather_fusion = bf16[144,128,128]{2,1,0:T(8,128)(2,1)} fusion(bf16[24,128,128]{2,1,0:T(8,128)(2,1)S(1)} %get-tuple-element.133, s32[1024]{0:T(1024)S(1)} %pad_clamp_fusion.2), kind=kCustom, calls=%fused_computation.1.clone.1 | custom fusion | bytes 9437760 | tf_op jit(solution)/shard_map/while/body/eval_jaxpr/gather | solution.py:31
  291.3 7.9 %fusion.38 = bf16[1,8,128,128]{3,2,1,0:T(8,128)(2,1)S(1)} fusion(bf16[8,18,128,128]{3,2,1,0:T(8,128)(2,1)} %bitcast.73, f32[8,128,18,128]{1,3,2,0:T(8,128)} %copy-done, f32[8,128]{1,0:T(8,128)S(1)} %get-tuple-element.138, pred[8,18]{1,0:T(8,128)(4,1)S(1)} %bitcast.86, f32[8,128]{1,0:T(8,128)S(1)} %fusion.37), kind=kOutput, calls=%fused_computation.12.clone.1 | convolution fusion | flops 616038400 | bytes 14426256 | tf_op jit(solution)/shard_map/while/body/eval_jaxpr/qtks,qksd->qtd/dot_general | solution.py:41
  305.3 7.6 %gather_fusion.1 = bf16[144,128,128]{2,1,0:T(8,128)(2,1)} fusion(bf16[24,128,128]{2,1,0:T(8,128)(2,1)S(1)} %get-tuple-element.136, s32[1024]{0:T(1024)S(1)} %pad_clamp_fusion.2), kind=kCustom, calls=%fused_computation.clone.1 | custom fusion | bytes 9437760 | tf_op jit(solution)/shard_map/while/body/eval_jaxpr/gather | solution.py:30
  312.9 3.4 fusion.36
  319.9 7.5 %gather_fusion = bf16[144,128,128]{2,1,0:T(8,128)(2,1)} fusion(bf16[24,128,128]{2,1,0:T(8,128)(2,1)S(1)} %get-tuple-element.133, s32[1024]{0:T(1024)S(1)} %pad_clamp_fusion.2), kind=kCustom, calls=%fused_computation.1.clone.1 | custom fusion | bytes 9437760 | tf_op jit(solution)/shard_map/while/body/eval_jaxpr/gather | solution.py:31
  327.4 7.9 %fusion.38 = bf16[1,8,128,128]{3,2,1,0:T(8,128)(2,1)S(1)} fusion(bf16[8,18,128,128]{3,2,1,0:T(8,128)(2,1)} %bitcast.73, f32[8,128,18,128]{1,3,2,0:T(8,128)} %copy-done, f32[8,128]{1,0:T(8,128)S(1)} %get-tuple-element.138, pred[8,18]{1,0:T(8,128)(4,1)S(1)} %bitcast.86, f32[8,128]{1,0:T(8,128)S(1)} %fusion.37), kind=kOutput, calls=%fused_computation.12.clone.1 | convolution fusion | flops 616038400 | bytes 14426256 | tf_op jit(solution)/shard_map/while/body/eval_jaxpr/qtks,qksd->qtd/dot_general | solution.py:41
  336.3 26.5 %all_to_all.68 = bf16[8,128,768]{1,2,0:T(8,128)(2,1)S(1)} all-to-all(bf16[8,128,768]{1,2,0:T(8,128)(2,1)} %bitcast.83), channel_id=1, replica_groups=mesh['ctx'=16,'head'=8] {'head'}, dimensions={0} | all-to-all | bytes 3145728 | tf_op jit(solution)/shard_map/all_to_all | solution.py:74
  (73 shorter events, 61.8 us)
Async XLA Ops:
  3.5 28.2 %all-to-all-start.1 = ((bf16[128,8,768]{2,0,1:T(8,128)(2,1)}), bf16[128,8,768]{2,0,1:T(8,128)(2,1)S(1)}, u32[]{:S(2)}, u32[]{:S(2)}) async-start(bf16[128,8,768]{2,0,1:T(8,128)(2,1)} %copy.23), calls=%async_computation.1 | async-start | bytes 3145728 | tf_op jit(solution)/shard_map/all_to_all | solution.py:52
  60.5 13.2 %collective-permute-start = (bf16[2,1024,768]{2,1,0:T(8,128)(2,1)}, bf16[2,1024,768]{2,1,0:T(8,128)(2,1)}, u32[]{:S(2)}, u32[]{:S(2)}) collective-permute-start(bf16[2,1024,768]{2,1,0:T(8,128)(2,1)} %pad_maximum_fusion.1), channel_id=1, source_target_pairs={{0,8},{8,16},{16,24},{24,32},{32,40},{40,48},{48,56},{56,64},{64,7... | collective-permute-start | bytes 9437192 | tf_op jit(solution)/shard_map/ppermute | solution.py:21
  63.4 10.3 %collective-permute-start.1 = (bf16[2,1024,768]{2,1,0:T(8,128)(2,1)}, bf16[2,1024,768]{2,1,0:T(8,128)(2,1)}, u32[]{:S(2)}, u32[]{:S(2)}) collective-permute-start(bf16[2,1024,768]{2,1,0:T(8,128)(2,1)} %pad_maximum_fusion.1), channel_id=1, source_target_pairs={{8,0},{16,8},{24,16},{32,24},{40,32},{48,40},{56,48},{64,56},{72,6... | collective-permute-start | bytes 9437192 | tf_op jit(solution)/shard_map/ppermute | solution.py:24
  67.3 51.9 %all-to-all-start = ((bf16[128,8,768]{0,2,1:T(8,128)(2,1)}), bf16[128,8,768]{0,2,1:T(8,128)(2,1)}, u32[]{:S(2)}, u32[]{:S(2)}) async-start(bf16[128,8,768]{0,2,1:T(8,128)(2,1)} %bitcast.79), calls=%async_computation | async-start | bytes 3145728 | tf_op jit(solution)/shard_map/all_to_all | solution.py:51
  135.3 3.6 %copy-start = (f32[8,128,18,128]{1,3,2,0:T(8,128)}, f32[8,128,18,128]{1,3,2,0:T(8,128)S(1)}, u32[]{:S(2)}) copy-start(f32[8,128,18,128]{1,3,2,0:T(8,128)S(1)} %get-tuple-element.137) | copy-start | bytes 28311556 | tf_op jit(solution)/shard_map/while
  171.5 3.6 %copy-start = (f32[8,128,18,128]{1,3,2,0:T(8,128)}, f32[8,128,18,128]{1,3,2,0:T(8,128)S(1)}, u32[]{:S(2)}) copy-start(f32[8,128,18,128]{1,3,2,0:T(8,128)S(1)} %get-tuple-element.137) | copy-start | bytes 28311556 | tf_op jit(solution)/shard_map/while
  207.7 3.6 %copy-start = (f32[8,128,18,128]{1,3,2,0:T(8,128)}, f32[8,128,18,128]{1,3,2,0:T(8,128)S(1)}, u32[]{:S(2)}) copy-start(f32[8,128,18,128]{1,3,2,0:T(8,128)S(1)} %get-tuple-element.137) | copy-start | bytes 28311556 | tf_op jit(solution)/shard_map/while
  243.9 3.6 %copy-start = (f32[8,128,18,128]{1,3,2,0:T(8,128)}, f32[8,128,18,128]{1,3,2,0:T(8,128)S(1)}, u32[]{:S(2)}) copy-start(f32[8,128,18,128]{1,3,2,0:T(8,128)S(1)} %get-tuple-element.137) | copy-start | bytes 28311556 | tf_op jit(solution)/shard_map/while
  280.1 3.6 %copy-start = (f32[8,128,18,128]{1,3,2,0:T(8,128)}, f32[8,128,18,128]{1,3,2,0:T(8,128)S(1)}, u32[]{:S(2)}) copy-start(f32[8,128,18,128]{1,3,2,0:T(8,128)S(1)} %get-tuple-element.137) | copy-start | bytes 28311556 | tf_op jit(solution)/shard_map/while
  316.3 3.6 %copy-start = (f32[8,128,18,128]{1,3,2,0:T(8,128)}, f32[8,128,18,128]{1,3,2,0:T(8,128)S(1)}, u32[]{:S(2)}) copy-start(f32[8,128,18,128]{1,3,2,0:T(8,128)S(1)} %get-tuple-element.137) | copy-start | bytes 28311556 | tf_op jit(solution)/shard_map/while
where the time goes:
time: 369 us; the launch traced here: 364 us
  local copies, waits for them, and re-layouts  125 us (34%)
  matrix products  68.1 us (18%)
  waiting for transfers between devices  54.3 us (15%)
  blocking collectives  53.3 us (14%)
  other arithmetic  31.4 us (9%)
  starting transfers between devices  18.7 us (5%)
  loops' own time  13.8 us (4%)
    dot_general x6, matrix products, attend_all(): jnp.einsum('qtks,qksd->qtd', probs, chosen_values, preferred_element_type...  47.6 us
    gather x6, local copies, waits for them, and re-layouts, attend_all(): chosen_keys = head_pairs[0][local_ids]  45.6 us
    gather x6, local copies, waits for them, and re-layouts, attend_all(): chosen_values = head_pairs[1][local_ids]  45.1 us
    all_to_all x1, waiting for transfers between devices, shards(): lax.all_to_all(queries, 'head', split_axis=1, concat_axis=0, tiled=True)  37.7 us
    all_to_all x1, blocking collectives, shards(): lax.all_to_all(value_rows, 'head', split_axis=1, concat_axis=0, tiled=True)  26.8 us
    all_to_all x1, blocking collectives, shards(): lax.all_to_all(regrouped, 'head', split_axis=0, concat_axis=1, tiled=True)  26.5 us
    dot_general x6, matrix products, attend_all(): jnp.einsum('qtd,qksd->qtks', head_query, chosen_keys, preferred_element_t...  20.5 us
    reduce_sum x6, other arithmetic, attend_all(): row_total = jnp.sum(weight, axis=(2, 3))  17.4 us
  transfers between devices with their start and end apart: 4, of which 2 were waited for; matrix products, arithmetic and copies ran while one was open for 4% of the time, Pallas kernels for 0%

commit v1 on v0

v1 whole, which is shorter than its diff:
```python
import functools
import math

import jax
import jax.numpy as jnp
from jax import lax
from jax.experimental import pallas as pl
from jax.experimental.pallas import tpu as pltpu
from jax.sharding import PartitionSpec as P

HDIM = 128
TILE = 128
MESH = pl.DeviceIdType.MESH
MASKED = -1e30
EXP2_SCALE = HDIM ** -0.5 / math.log(2.0)


def attend(tiles_ref, qb, work, sc, ob, j, t, base, own):
    slots = tiles_ref.shape[2]
    query = qb[j, t]
    ids, bias = [], []
    for s in range(slots):
        listed = tiles_ref[j, t, s]
        live = listed >= 0
        ids.append(jnp.clip(jnp.where(live, listed - base, own), 0, 3 * own - 1))
        bias.append(jnp.where(live, 0.0, MASKED))
    top = None
    for s in range(0, slots, 2):
        keys = jnp.concatenate([work[0, ids[s]], work[0, ids[s + 1]]], axis=0)
        scores = lax.dot_general(query, keys, (((1,), (1,)), ((), ())), preferred_element_type=jnp.float32)
        first = scores[:, :TILE] + bias[s]
        second = scores[:, TILE:] + bias[s + 1]
        sc[s] = first
        sc[s + 1] = second
        pair = jnp.maximum(first, second)
        top = pair if top is None else jnp.maximum(top, pair)
    row_max = jnp.max(top, axis=1, keepdims=True)
    total, numerator = None, None
    for s in range(0, slots, 2):
        first = jnp.exp2((sc[s] - row_max) * EXP2_SCALE)
        second = jnp.exp2((sc[s + 1] - row_max) * EXP2_SCALE)
        pair = first + second
        total = pair if total is None else total + pair
        probs = jnp.concatenate([first.astype(jnp.bfloat16), second.astype(jnp.bfloat16)], axis=1)
        values = jnp.concatenate([work[1, ids[s]], work[1, ids[s + 1]]], axis=0)
        part = jnp.dot(probs, values, preferred_element_type=jnp.float32)
        numerator = part if numerator is None else numerator + part
    row_total = jnp.sum(total, axis=1, keepdims=True)
    ob[j, t] = (numerator / row_total).astype(jnp.bfloat16)


def kernel(n_ctx, n_head, tiles_ref, q_ref, k_ref, v_ref, out_ref, qb, kvb, ob, work, sc, send_in, send_halo, send_out, recv_kv, recv_q, recv_halo, recv_out):
    heads = tiles_ref.shape[0]
    c, me = lax.axis_index("ctx"), lax.axis_index("head")
    before, after = lax.rem(c + n_ctx - 1, n_ctx), lax.rem(c + 1, n_ctx)
    base = (c - 1) * n_head

    def columns(group, j):
        return pl.ds(pl.multiple_of((group * heads + j) * HDIM, HDIM), HDIM)

    barrier = pltpu.get_barrier_semaphore()
    for p in range(1, n_head):
        pl.semaphore_signal(barrier, inc=1, device_id=(c, lax.rem(me + p, n_head)), device_id_type=MESH)
    for other in (before, after):
        pl.semaphore_signal(barrier, inc=1, device_id=(other, me), device_id_type=MESH)
    pl.semaphore_wait(barrier, n_head + 1)

    def send_tile(source, place, j, sem_index, recv):
        for p in range(1, n_head):
            peer = lax.rem(me + p, n_head)
            pltpu.make_async_remote_copy(
                src_ref=source.at[:, columns(peer, j)], dst_ref=place(), send_sem=send_in.at[sem_index],
                recv_sem=recv, device_id=(c, peer), device_id_type=MESH,
            ).start()
        pltpu.make_async_copy(source.at[:, columns(me, j)], place(), recv).start()

    def send_kv(j):
        send_tile(k_ref, lambda: kvb.at[j, 0, n_head + me], j, 0, recv_kv.at[j])
        send_tile(v_ref, lambda: kvb.at[j, 1, n_head + me], j, 1, recv_kv.at[j])

    def send_q(j):
        send_tile(q_ref, lambda: qb.at[j, me], j, 2, recv_q.at[j])

    send_kv(0)

    @pl.loop(0, heads)
    def _(j):
        @pl.when(j + 1 < heads)
        def _():
            send_kv(j + 1)

        send_q(j)

    def pass_halo(j):
        own = kvb.at[j, :, pl.ds(n_head, n_head)]
        pltpu.make_async_copy(own, own, recv_kv.at[j]).wait()
        for other, slot in ((after, 0), (before, 2 * n_head)):
            pltpu.make_async_remote_copy(
                src_ref=own, dst_ref=kvb.at[j, :, pl.ds(slot, n_head)], send_sem=send_halo,
                recv_sem=recv_halo.at[j], device_id=(other, me), device_id_type=MESH,
            ).start()

    def return_tile(j, t):
        place = out_ref.at[:, columns(me, j)]

        @pl.when(t == me)
        def _():
            pltpu.make_async_copy(ob.at[j, t], place, recv_out).start()

        @pl.when(t != me)
        def _():
            pltpu.make_async_remote_copy(
                src_ref=ob.at[j, t], dst_ref=place, send_sem=send_out,
                recv_sem=recv_out, device_id=(c, t), device_id_type=MESH,
            ).start()

    pass_halo(0)

    @pl.loop(0, heads)
    def _(j):
        @pl.when(j + 1 < heads)
        def _():
            pass_halo(j + 1)

        both = kvb.at[j, :, pl.ds(0, 2 * n_head)]
        pltpu.make_async_copy(both, both, recv_halo.at[j]).wait()
        pltpu.make_async_copy(qb.at[j], qb.at[j], recv_q.at[j]).wait()

        @pl.loop(0, 3 * n_head)
        def _(i):
            work[0, i] = kvb[j, 0, i]
            work[1, i] = kvb[j, 1, i]

        @pl.loop(0, n_head)
        def _(i):
            t = lax.rem(me + 1 + i, n_head)
            attend(tiles_ref, qb, work, sc, ob, j, t, base, n_head)

            @pl.when(i > 0)
            def _():
                return_tile(j, lax.rem(me + i, n_head))

        return_tile(j, me)

    sent = qb.at[:, pl.ds(0, n_head - 1)]
    for i in range(3):
        pltpu.make_async_copy(sent, sent, send_in.at[i]).wait()
    halo = kvb.at[:, :, pl.ds(0, 2 * n_head)]
    pltpu.make_async_copy(halo, halo, send_halo).wait()
    pltpu.make_async_copy(sent, sent, send_out).wait()
    pltpu.make_async_copy(out_ref, out_ref, recv_out).wait()


def solution(mesh):
    n_ctx, n_head = mesh.shape["ctx"], mesh.shape["head"]

    def shards(queries, key_rows, value_rows, key_tiles):
        heads, _, slots = key_tiles.shape
        return pl.pallas_call(
            functools.partial(kernel, n_ctx, n_head),
            out_shape=jax.ShapeDtypeStruct(queries.shape, queries.dtype),
            in_specs=[pl.BlockSpec(memory_space=pltpu.SMEM)] + [pl.BlockSpec(memory_space=pltpu.HBM)] * 3,
            out_specs=pl.BlockSpec(memory_space=pltpu.HBM),
            scratch_shapes=[
                pltpu.VMEM((heads, n_head, TILE, HDIM), jnp.bfloat16),
                pltpu.VMEM((heads, 2, 3 * n_head, TILE, HDIM), jnp.bfloat16),
                pltpu.VMEM((heads, n_head, TILE, HDIM), jnp.bfloat16),
                pltpu.VMEM((2, 3 * n_head, TILE, HDIM), jnp.bfloat16),
                pltpu.VMEM((slots, TILE, TILE), jnp.float32),
                pltpu.SemaphoreType.DMA((3,)),
                pltpu.SemaphoreType.DMA,
                pltpu.SemaphoreType.DMA,
                pltpu.SemaphoreType.DMA((heads,)),
                pltpu.SemaphoreType.DMA((heads,)),
                pltpu.SemaphoreType.DMA((heads,)),
                pltpu.SemaphoreType.DMA,
            ],
            compiler_params=pltpu.CompilerParams(
                collective_id=0, has_side_effects=True, vmem_limit_bytes=48 * 1024 * 1024
            ),
        )(key_tiles, queries, key_rows, value_rows)

    return jax.shard_map(
        shards,
        mesh=mesh,
        in_specs=(P(("ctx", "head"), None), P(("ctx", "head"), None), P(("ctx", "head"), None), P("head", "ctx", None)),
        out_specs=P(("ctx", "head"), None),
        check_vma=False,
    )
```

time: 369 us -> 132 us (0.36); the launches traced: 364 us -> 132 us
  Pallas kernels: 0 us -> 127 us
  local copies, waits for them, and re-layouts: 125 us -> 4.7 us
  matrix products: 68.1 us -> 0 us
  waiting for transfers between devices: 54.3 us -> 0 us
  blocking collectives: 53.3 us -> 0 us
  other arithmetic: 31.4 us -> 0 us
  starting transfers between devices: 18.7 us -> 0 us
  loops' own time: 13.8 us -> 0 us
    pallas_call x0 -> x1, Pallas kernels: none -> 127 us  [shards(): pl.pallas_call(functools.partial(kernel, n_ctx, n_head), out_shape=jax.Sh...]
    gather x12 -> x0, local copies, waits for them, and re-layouts: 90.7 us -> none  [the longest x6 45.6 us: attend_all(): chosen_keys = head_pairs[0][local_ids]]
    dot_general x12 -> x0, matrix products: 68.1 us -> none  [the longest x6 47.6 us: attend_all(): jnp.einsum('qtks,qksd->qtd', probs, chosen_values, preferred_element_type...]
    all_to_all x2 -> x0, waiting for transfers between devices: 54.3 us -> none  [the longest x1 37.7 us: shards(): lax.all_to_all(queries, 'head', split_axis=1, concat_axis=0, tiled=True)]
    all_to_all x2 -> x0, blocking collectives: 53.3 us -> none  [the longest x1 26.8 us: shards(): lax.all_to_all(value_rows, 'head', split_axis=1, concat_axis=0, tiled=True)]
    reduce_sum x6 -> x0, other arithmetic: 17.4 us -> none  [attend_all(): row_total = jnp.sum(weight, axis=(2, 3))]
    all_to_all x2 -> x0, starting transfers between devices: 14.5 us -> none  [the longest x1 8.09 us: shards(): lax.all_to_all(key_rows, 'head', split_axis=1, concat_axis=0, tiled=True)]
    another operation x1 -> x0, loops' own time: 13.8 us -> none  [shards(): result = lax.map(one_head, jnp.arange(heads_dev, dtype=jnp.int32))]
  transfers between devices with their start and end apart: 4 -> 0, of which waited for: 2 -> 0; matrix products, arithmetic and copies ran while one was open for 4% -> 0% of each run, Pallas kernels for 0% -> 0%
where the time goes in v1:
time: 132 us
  Pallas kernels  127 us (96%)
  local copies, waits for them, and re-layouts  4.7 us (4%)
    pallas_call x1, Pallas kernels, shards(): pl.pallas_call(functools.partial(kernel, n_ctx, n_head), out_shape=jax.Sh...  127 us
    unnamed x7, local copies, waits for them, and re-layouts  4.7 us

profile of v1, /device:TPU:6, one launch (start us, length us, event | category | flops | bytes accessed | tf_op | source)
XLA Modules:
  0.0 132.1 jit_solution(14476417181940165995)
XLA Ops:
  0.0 0.0 copy-start
  0.0 1.4 %copy-done = bf16[128,6144]{1,0:T(8,128)(2,1)S(1)} copy-done((bf16[128,6144]{1,0:T(8,128)(2,1)S(1)}, bf16[128,6144]{1,0:T(8,128)(2,1)}, u32[]{:S(2)}) %copy-start) | copy-done | bytes 1572888
  1.4 0.0 copy-start.1
  1.4 1.4 %copy-done.1 = bf16[128,6144]{1,0:T(8,128)(2,1)S(1)} copy-done((bf16[128,6144]{1,0:T(8,128)(2,1)S(1)}, bf16[128,6144]{1,0:T(8,128)(2,1)}, u32[]{:S(2)}) %copy-start.1) | copy-done | bytes 1572888
  2.8 0.0 copy-start.2
  2.8 0.7 copy-done.2
  3.6 127.4 %shard_map.46 = bf16[128,6144]{1,0:T(8,128)(2,1)S(1)} custom-call(s32[6,8,18]{2,1,0:T(8,128)S(1)} %copy-done.2, bf16[128,6144]{1,0:T(8,128)(2,1)S(1)} %copy-done, bf16[128,6144]{1,0:T(8,128)(2,1)S(1)} %copy-done.1, bf16[128,6144]{1,0:T(8,128)(2,1)} %v_ref.1), custom_call_target="tpu_custom_call" | custom-call | tf_op jit(solution)/shard_map/pallas_call | solution.py:159
  130.9 1.1 copy.6
Async XLA Ops:
  0.0 1.4 %copy-start = (bf16[128,6144]{1,0:T(8,128)(2,1)S(1)}, bf16[128,6144]{1,0:T(8,128)(2,1)}, u32[]{:S(2)}) copy-start(bf16[128,6144]{1,0:T(8,128)(2,1)} %q_ref.1) | copy-start | bytes 4718596
  1.4 1.4 %copy-start.1 = (bf16[128,6144]{1,0:T(8,128)(2,1)S(1)}, bf16[128,6144]{1,0:T(8,128)(2,1)}, u32[]{:S(2)}) copy-start(bf16[128,6144]{1,0:T(8,128)(2,1)} %k_ref.1) | copy-start | bytes 4718596
  2.8 0.7 copy-start.2

commit v2 on v1

--- a/solution.py
+++ b/solution.py
@@ -49,21 +49,32 @@
     ob[j, t] = (numerator / row_total).astype(jnp.bfloat16)
 
 
-def kernel(n_ctx, n_head, tiles_ref, q_ref, k_ref, v_ref, out_ref, qb, kvb, ob, work, sc, send_in, send_halo, send_out, recv_kv, recv_q, recv_halo, recv_out):
+def kernel(n_ctx, n_head, tiles_ref, q_ref, k_ref, v_ref, out_ref, qb, kvb, ob, work, sc, send_in, send_across_sem, send_halo, send_out, recv_kv, recv_q, recv_below, recv_above, recv_out):
     heads = tiles_ref.shape[0]
     c, me = lax.axis_index("ctx"), lax.axis_index("head")
-    before, after = lax.rem(c + n_ctx - 1, n_ctx), lax.rem(c + 1, n_ctx)
     base = (c - 1) * n_head
+    turn, last = n_ctx // 2, n_ctx - 1
+    own, above = n_head, 2 * n_head
+    at_end, at_turn = (c == 0) | (c == last), (c == turn - 1) | (c == turn)
 
     def columns(group, j):
         return pl.ds(pl.multiple_of((group * heads + j) * HDIM, HDIM), HDIM)
 
+    def greet(ctx, head):
+        pl.semaphore_signal(barrier, inc=1, device_id=(ctx, head), device_id_type=MESH)
+
     barrier = pltpu.get_barrier_semaphore()
     for p in range(1, n_head):
-        pl.semaphore_signal(barrier, inc=1, device_id=(c, lax.rem(me + p, n_head)), device_id_type=MESH)
-    for other in (before, after):
-        pl.semaphore_signal(barrier, inc=1, device_id=(other, me), device_id_type=MESH)
-    pl.semaphore_wait(barrier, n_head + 1)
+        greet(c, lax.rem(me + p, n_head))
+    pl.when((c != 0) & (c != turn))(lambda: greet(c - 1, me))
+    pl.when((c != last) & (c != turn - 1))(lambda: greet(c + 1, me))
+
+    @pl.when(at_turn)
+    def _():
+        for group in range(n_head):
+            greet(2 * turn - 1 - c, group)
+
+    pl.semaphore_wait(barrier, jnp.where(at_end, n_head, jnp.where(at_turn, 2 * n_head, n_head + 1)))
 
     def send_tile(source, place, j, sem_index, recv):
         for p in range(1, n_head):
@@ -74,9 +85,20 @@
             ).start()
         pltpu.make_async_copy(source.at[:, columns(me, j)], place(), recv).start()
 
+    def send_across(j, ctx, first, recv):
+        for i, source in enumerate((k_ref, v_ref)):
+            for p in range(n_head):
+                group = lax.rem(me + p, n_head)
+                pltpu.make_async_remote_copy(
+                    src_ref=source.at[:, columns(group, j)], dst_ref=kvb.at[j, i, first + me], send_sem=send_across_sem.at[i],
+                    recv_sem=recv.at[j], device_id=(ctx, group), device_id_type=MESH,
+                ).start()
+
     def send_kv(j):
         send_tile(k_ref, lambda: kvb.at[j, 0, n_head + me], j, 0, recv_kv.at[j])
         send_tile(v_ref, lambda: kvb.at[j, 1, n_head + me], j, 1, recv_kv.at[j])
+        pl.when(c == turn - 1)(lambda: send_across(j, turn, 0, recv_below))
+        pl.when(c == turn)(lambda: send_across(j, turn - 1, above, recv_above))
 
     def send_q(j):
         send_tile(q_ref, lambda: qb.at[j, me], j, 2, recv_q.at[j])
@@ -91,14 +113,20 @@
 
         send_q(j)
 
+    def push(j, source, place, count, ctx, recv):
+        pltpu.make_async_remote_copy(
+            src_ref=kvb.at[j, :, pl.ds(source, count)], dst_ref=kvb.at[j, :, pl.ds(place, count)],
+            send_sem=send_halo, recv_sem=recv.at[j], device_id=(ctx, me), device_id_type=MESH,
+        ).start()
+
+    def landed(j, first, recv):
+        slab = kvb.at[j, :, pl.ds(first, n_head)]
+        pltpu.make_async_copy(slab, slab, recv.at[j]).wait()
+
     def pass_halo(j):
-        own = kvb.at[j, :, pl.ds(n_head, n_head)]
-        pltpu.make_async_copy(own, own, recv_kv.at[j]).wait()
-        for other, slot in ((after, 0), (before, 2 * n_head)):
-            pltpu.make_async_remote_copy(
-                src_ref=own, dst_ref=kvb.at[j, :, pl.ds(slot, n_head)], send_sem=send_halo,
-                recv_sem=recv_halo.at[j], device_id=(other, me), device_id_type=MESH,
-            ).start()
+        landed(j, own, recv_kv)
+        pl.when((c != 0) & (c != turn))(lambda: push(j, own, above, n_head, c - 1, recv_above))
+        pl.when((c != last) & (c != turn - 1))(lambda: push(j, own, 0, n_head, c + 1, recv_below))
 
     def return_tile(j, t):
         place = out_ref.at[:, columns(me, j)]
@@ -122,8 +150,8 @@
         def _():
             pass_halo(j + 1)
 
-        both = kvb.at[j, :, pl.ds(0, 2 * n_head)]
-        pltpu.make_async_copy(both, both, recv_halo.at[j]).wait()
+        pl.when(c != 0)(lambda: landed(j, 0, recv_below))
+        pl.when(c != last)(lambda: landed(j, above, recv_above))
         pltpu.make_async_copy(qb.at[j], qb.at[j], recv_q.at[j]).wait()
 
         @pl.loop(0, 3 * n_head)
@@ -145,8 +173,15 @@
     sent = qb.at[:, pl.ds(0, n_head - 1)]
     for i in range(3):
         pltpu.make_async_copy(sent, sent, send_in.at[i]).wait()
-    halo = kvb.at[:, :, pl.ds(0, 2 * n_head)]
+    halo = kvb.at[:, :, pl.ds(0, n_head)]
     pltpu.make_async_copy(halo, halo, send_halo).wait()
+    pl.when(~(at_end | at_turn))(lambda: pltpu.make_async_copy(halo, halo, send_halo).wait())
+
+    @pl.when(at_turn)
+    def _():
+        for i in range(2):
+            pltpu.make_async_copy(qb, qb, send_across_sem.at[i]).wait()
+
     pltpu.make_async_copy(sent, sent, send_out).wait()
     pltpu.make_async_copy(out_ref, out_ref, recv_out).wait()
 
@@ -168,15 +203,17 @@
                 pltpu.VMEM((2, 3 * n_head, TILE, HDIM), jnp.bfloat16),
                 pltpu.VMEM((slots, TILE, TILE), jnp.float32),
                 pltpu.SemaphoreType.DMA((3,)),
+                pltpu.SemaphoreType.DMA((2,)),
                 pltpu.SemaphoreType.DMA,
                 pltpu.SemaphoreType.DMA,
+                pltpu.SemaphoreType.DMA((heads,)),
                 pltpu.SemaphoreType.DMA((heads,)),
                 pltpu.SemaphoreType.DMA((heads,)),
                 pltpu.SemaphoreType.DMA((heads,)),
                 pltpu.SemaphoreType.DMA,
             ],
             compiler_params=pltpu.CompilerParams(
-                collective_id=0, has_side_effects=True, vmem_limit_bytes=48 * 1024 * 1024
+                collective_id=0, has_side_effects=True, vmem_limit_bytes=67043328
             ),
         )(key_tiles, queries, key_rows, value_rows)
 

time: 132 us -> 116 us (0.88)
  the two profiles are of different devices: /device:TPU:6 before, /device:TPU:56 now
where the time goes in v2:
time: 116 us; the launch traced here: 115 us
  Pallas kernels  113 us (97%)
  local copies, waits for them, and re-layouts  2.69 us (2%)
    pallas_call x1, Pallas kernels, shards(): pl.pallas_call(functools.partial(kernel, n_ctx, n_head), out_shape=jax.Sh...  113 us
    unnamed x1, local copies, waits for them, and re-layouts  2.69 us

profile of v2, /device:TPU:56, one launch (start us, length us, event | category | flops | bytes accessed | tf_op | source)
XLA Modules:
  0.0 115.5 jit_solution(16791505978398420529)
XLA Ops:
  0.0 112.8 %shard_map.46 = bf16[128,6144]{1,0:T(8,128)(2,1)} custom-call(s32[6,8,18]{2,1,0:T(8,128)} %tiles_ref.1, bf16[128,6144]{1,0:T(8,128)(2,1)} %q_ref.1, bf16[128,6144]{1,0:T(8,128)(2,1)} %k_ref.1, bf16[128,6144]{1,0:T(8,128)(2,1)} %v_ref.1), custom_call_target="tpu_custom_call" | custom-call | tf_op jit(solution)/shard_map/pallas_call | solution.py:194
  112.8 2.7 %copy.6 = bf16[128,6144]{1,0:T(8,128)(2,1)} copy(bf16[128,6144]{1,0:T(8,128)(2,1)} %shard_map.46) | data formatting | bytes 3145728

commit v3 on v2

--- a/solution.py
+++ b/solution.py
@@ -15,30 +15,34 @@
 EXP2_SCALE = HDIM ** -0.5 / math.log(2.0)
 
 
-def attend(tiles_ref, qb, work, sc, ob, j, t, base, own):
-    slots = tiles_ref.shape[2]
-    query = qb[j, t]
+def listed_tiles(tiles_ref, j, t, base, own):
     ids, bias = [], []
-    for s in range(slots):
+    for s in range(tiles_ref.shape[2]):
         listed = tiles_ref[j, t, s]
         live = listed >= 0
-        ids.append(jnp.clip(jnp.where(live, listed - base, own), 0, 3 * own - 1))
+        ids.append(jnp.clip(jnp.where(live, listed - base, own + t), 0, 3 * own - 1))
         bias.append(jnp.where(live, 0.0, MASKED))
+    return ids, bias
+
+
+def score(qb, work, sc, ids, j, t):
+    query = qb[j, t]
     top = None
-    for s in range(0, slots, 2):
+    for s in range(0, len(ids), 2):
         keys = jnp.concatenate([work[0, ids[s]], work[0, ids[s + 1]]], axis=0)
         scores = lax.dot_general(query, keys, (((1,), (1,)), ((), ())), preferred_element_type=jnp.float32)
-        first = scores[:, :TILE] + bias[s]
-        second = scores[:, TILE:] + bias[s + 1]
-        sc[s] = first
-        sc[s + 1] = second
-        pair = jnp.maximum(first, second)
+        sc[s] = scores[:, :TILE]
+        sc[s + 1] = scores[:, TILE:]
+        pair = jnp.maximum(scores[:, :TILE], scores[:, TILE:])
         top = pair if top is None else jnp.maximum(top, pair)
-    row_max = jnp.max(top, axis=1, keepdims=True)
+    return jnp.max(top, axis=1, keepdims=True)
+
+
+def gather(work, sc, pb, ob, ids, bias, row_max, j, t):
     total, numerator = None, None
-    for s in range(0, slots, 2):
-        first = jnp.exp2((sc[s] - row_max) * EXP2_SCALE)
-        second = jnp.exp2((sc[s + 1] - row_max) * EXP2_SCALE)
+    for s in range(0, len(ids), 2):
+        first = jnp.exp2((sc[s] - row_max) * EXP2_SCALE + bias[s])
+        second = jnp.exp2((sc[s + 1] - row_max) * EXP2_SCALE + bias[s + 1])
         pair = first + second
         total = pair if total is None else total + pair
         probs = jnp.concatenate([first.astype(jnp.bfloat16), second.astype(jnp.bfloat16)], axis=1)
@@ -49,7 +53,7 @@
     ob[j, t] = (numerator / row_total).astype(jnp.bfloat16)
 
 
-def kernel(n_ctx, n_head, tiles_ref, q_ref, k_ref, v_ref, out_ref, qb, kvb, ob, work, sc, send_in, send_across_sem, send_halo, send_out, recv_kv, recv_q, recv_below, recv_above, recv_out):
+def kernel(n_ctx, n_head, tiles_ref, q_ref, k_ref, v_ref, out_ref, qb, kvb, ob, work, sc, pb, send_in, send_across_sem, send_halo, send_out, recv_kv, recv_q, recv_below, recv_above, recv_out):
     heads = tiles_ref.shape[0]
     c, me = lax.axis_index("ctx"), lax.axis_index("head")
     base = (c - 1) * n_head
@@ -159,15 +163,20 @@
             work[0, i] = kvb[j, 0, i]
             work[1, i] = kvb[j, 1, i]
 
-        @pl.loop(0, n_head)
+        @pl.loop(0, n_head, step=2)
         def _(i):
-            t = lax.rem(me + 1 + i, n_head)
-            attend(tiles_ref, qb, work, sc, ob, j, t, base, n_head)
+            tiles = [lax.rem(me + 1 + i + k, n_head) for k in range(2)]
+            lists = [listed_tiles(tiles_ref, j, t, base, n_head) for t in tiles]
+            tops = [score(qb, work, sc.at[k], lists[k][0], j, tiles[k]) for k in range(2)]
+            for k in range(2):
+                gather(work, sc.at[k], pb.at[k], ob, *lists[k], tops[k], j, tiles[k])
 
             @pl.when(i > 0)
             def _():
-                return_tile(j, lax.rem(me + i, n_head))
-
+                for k in range(2):
+                    return_tile(j, lax.rem(me - 1 + i + k, n_head))
+
+        return_tile(j, lax.rem(me + n_head - 1, n_head))
         return_tile(j, me)
 
     sent = qb.at[:, pl.ds(0, n_head - 1)]
@@ -201,7 +210,8 @@
                 pltpu.VMEM((heads, 2, 3 * n_head, TILE, HDIM), jnp.bfloat16),
                 pltpu.VMEM((heads, n_head, TILE, HDIM), jnp.bfloat16),
                 pltpu.VMEM((2, 3 * n_head, TILE, HDIM), jnp.bfloat16),
-                pltpu.VMEM((slots, TILE, TILE), jnp.float32),
+                pltpu.VMEM((2, slots, TILE, TILE), jnp.float32),
+                pltpu.VMEM((2, TILE, slots * TILE), jnp.bfloat16),
                 pltpu.SemaphoreType.DMA((3,)),
                 pltpu.SemaphoreType.DMA((2,)),
                 pltpu.SemaphoreType.DMA,

time: 116 us -> 109 us (0.940)
  the two profiles are of different devices: /device:TPU:56 before, /device:TPU:49 now
where the time goes in v3:
time: 109 us
  Pallas kernels  106 us (97%)
  local copies, waits for them, and re-layouts  2.69 us (2%)
    pallas_call x1, Pallas kernels, shards(): pl.pallas_call(functools.partial(kernel, n_ctx, n_head), out_shape=jax.Sh...  106 us
    unnamed x1, local copies, waits for them, and re-layouts  2.69 us

profile of v3, /device:TPU:49, one launch (start us, length us, event | category | flops | bytes accessed | tf_op | source)
XLA Modules:
  0.0 108.8 jit_solution(5771898760403808782)
XLA Ops:
  0.0 106.1 %shard_map.46 = bf16[128,6144]{1,0:T(8,128)(2,1)} custom-call(s32[6,8,18]{2,1,0:T(8,128)} %tiles_ref.1, bf16[128,6144]{1,0:T(8,128)(2,1)} %q_ref.1, bf16[128,6144]{1,0:T(8,128)(2,1)} %k_ref.1, bf16[128,6144]{1,0:T(8,128)(2,1)} %v_ref.1), custom_call_target="tpu_custom_call" | custom-call | tf_op jit(solution)/shard_map/pallas_call | solution.py:203
  106.1 2.7 %copy.6 = bf16[128,6144]{1,0:T(8,128)(2,1)} copy(bf16[128,6144]{1,0:T(8,128)(2,1)} %shard_map.46) | data formatting | bytes 3145728

commit v4 on v3

--- a/solution.py
+++ b/solution.py
@@ -38,7 +38,7 @@
     return jnp.max(top, axis=1, keepdims=True)
 
 
-def gather(work, sc, pb, ob, ids, bias, row_max, j, t):
+def gather(work, sc, ob, ids, bias, row_max, j, t):
     total, numerator = None, None
     for s in range(0, len(ids), 2):
         first = jnp.exp2((sc[s] - row_max) * EXP2_SCALE + bias[s])
@@ -53,13 +53,16 @@
     ob[j, t] = (numerator / row_total).astype(jnp.bfloat16)
 
 
-def kernel(n_ctx, n_head, tiles_ref, q_ref, k_ref, v_ref, out_ref, qb, kvb, ob, work, sc, pb, send_in, send_across_sem, send_halo, send_out, recv_kv, recv_q, recv_below, recv_above, recv_out):
+def kernel(n_ctx, n_head, tiles_ref, q_ref, k_ref, v_ref, out_ref, qb, kvb, passing, ob, work, sc, send_in, send_across_sem, send_halo, send_passing, send_out, recv_kv, recv_q, recv_below, recv_above, recv_passing, recv_out):
     heads = tiles_ref.shape[0]
     c, me = lax.axis_index("ctx"), lax.axis_index("head")
     base = (c - 1) * n_head
     turn, last = n_ctx // 2, n_ctx - 1
-    own, above = n_head, 2 * n_head
+    own, above, part = n_head, 2 * n_head, n_head // 2
+    via = ((turn // 2 - 1, 0), (turn // 2, part))
     at_end, at_turn = (c == 0) | (c == last), (c == turn - 1) | (c == turn)
+    at_via = functools.reduce(jnp.logical_or, [c == plane + place for plane in (0, turn) for place, _ in via])
+    far_plane = jnp.where(c < turn, turn, 0)
 
     def columns(group, j):
         return pl.ds(pl.multiple_of((group * heads + j) * HDIM, HDIM), HDIM)
@@ -77,8 +80,17 @@
     def _():
         for group in range(n_head):
             greet(2 * turn - 1 - c, group)
-
-    pl.semaphore_wait(barrier, jnp.where(at_end, n_head, jnp.where(at_turn, 2 * n_head, n_head + 1)))
+        for place, _ in via:
+            greet(place, me)
+            greet(turn + place, me)
+
+    @pl.when(at_via)
+    def _():
+        greet(turn - 1, me)
+        greet(turn, me)
+
+    greeted = jnp.where(at_end, n_head, jnp.where(at_turn, 2 * n_head + 4, jnp.where(at_via, n_head + 3, n_head + 1)))
+    pl.semaphore_wait(barrier, greeted)
 
     def send_tile(source, place, j, sem_index, recv):
         for p in range(1, n_head):
@@ -90,13 +102,12 @@
         pltpu.make_async_copy(source.at[:, columns(me, j)], place(), recv).start()
 
     def send_across(j, ctx, first, recv):
-        for i, source in enumerate((k_ref, v_ref)):
-            for p in range(n_head):
-                group = lax.rem(me + p, n_head)
-                pltpu.make_async_remote_copy(
-                    src_ref=source.at[:, columns(group, j)], dst_ref=kvb.at[j, i, first + me], send_sem=send_across_sem.at[i],
-                    recv_sem=recv.at[j], device_id=(ctx, group), device_id_type=MESH,
-                ).start()
+        for p in range(n_head):
+            group = lax.rem(me + p, n_head)
+            pltpu.make_async_remote_copy(
+                src_ref=k_ref.at[:, columns(group, j)], dst_ref=kvb.at[j, 0, first + me], send_sem=send_across_sem,
+                recv_sem=recv.at[j], device_id=(ctx, group), device_id_type=MESH,
+            ).start()
 
     def send_kv(j):
         send_tile(k_ref, lambda: kvb.at[j, 0, n_head + me], j, 0, recv_kv.at[j])
@@ -129,8 +140,28 @@
 
     def pass_halo(j):
         landed(j, own, recv_kv)
+
+        @pl.when(at_turn)
+        def _():
+            for place, first in via:
+                pltpu.make_async_remote_copy(
+                    src_ref=kvb.at[j, 1, pl.ds(own + first, part)], dst_ref=passing.at[j], send_sem=send_halo,
+                    recv_sem=recv_passing.at[j], device_id=(far_plane + place, me), device_id_type=MESH,
+                ).start()
+
         pl.when((c != 0) & (c != turn))(lambda: push(j, own, above, n_head, c - 1, recv_above))
         pl.when((c != last) & (c != turn - 1))(lambda: push(j, own, 0, n_head, c + 1, recv_below))
+
+    def relay(j):
+        for plane, target, shift, recv in ((0, turn - 1, above, recv_above), (turn, turn, 0, recv_below)):
+            for place, first in via:
+                @pl.when(c == plane + place)
+                def _():
+                    pltpu.make_async_copy(passing.at[j], passing.at[j], recv_passing.at[j]).wait()
+                    pltpu.make_async_remote_copy(
+                        src_ref=passing.at[j], dst_ref=kvb.at[j, 1, pl.ds(shift + first, part)], send_sem=send_passing,
+                        recv_sem=recv.at[j], device_id=(target, me), device_id_type=MESH,
+                    ).start()
 
     def return_tile(j, t):
         place = out_ref.at[:, columns(me, j)]
@@ -147,6 +178,7 @@
             ).start()
 
     pass_halo(0)
+    relay(0)
 
     @pl.loop(0, heads)
     def _(j):
@@ -169,7 +201,11 @@
             lists = [listed_tiles(tiles_ref, j, t, base, n_head) for t in tiles]
             tops = [score(qb, work, sc.at[k], lists[k][0], j, tiles[k]) for k in range(2)]
             for k in range(2):
-                gather(work, sc.at[k], pb.at[k], ob, *lists[k], tops[k], j, tiles[k])
+                gather(work, sc.at[k], ob, *lists[k], tops[k], j, tiles[k])
+
+            @pl.when((i == 4) & (j + 1 < heads))
+            def _():
+                relay(j + 1)
 
             @pl.when(i > 0)
             def _():
@@ -182,15 +218,16 @@
     sent = qb.at[:, pl.ds(0, n_head - 1)]
     for i in range(3):
         pltpu.make_async_copy(sent, sent, send_in.at[i]).wait()
-    halo = kvb.at[:, :, pl.ds(0, n_head)]
+    halo, half = kvb.at[:, :, pl.ds(0, n_head)], kvb.at[:, 0, pl.ds(0, n_head)]
     pltpu.make_async_copy(halo, halo, send_halo).wait()
     pl.when(~(at_end | at_turn))(lambda: pltpu.make_async_copy(halo, halo, send_halo).wait())
 
     @pl.when(at_turn)
     def _():
-        for i in range(2):
-            pltpu.make_async_copy(qb, qb, send_across_sem.at[i]).wait()
-
+        pltpu.make_async_copy(half, half, send_halo).wait()
+        pltpu.make_async_copy(qb, qb, send_across_sem).wait()
+
+    pl.when(at_via)(lambda: pltpu.make_async_copy(passing, passing, send_passing).wait())
     pltpu.make_async_copy(sent, sent, send_out).wait()
     pltpu.make_async_copy(out_ref, out_ref, recv_out).wait()
 
@@ -208,14 +245,16 @@
             scratch_shapes=[
                 pltpu.VMEM((heads, n_head, TILE, HDIM), jnp.bfloat16),
                 pltpu.VMEM((heads, 2, 3 * n_head, TILE, HDIM), jnp.bfloat16),
+                pltpu.VMEM((heads, n_head // 2, TILE, HDIM), jnp.bfloat16),
                 pltpu.VMEM((heads, n_head, TILE, HDIM), jnp.bfloat16),
                 pltpu.VMEM((2, 3 * n_head, TILE, HDIM), jnp.bfloat16),
                 pltpu.VMEM((2, slots, TILE, TILE), jnp.float32),
-                pltpu.VMEM((2, TILE, slots * TILE), jnp.bfloat16),
                 pltpu.SemaphoreType.DMA((3,)),
-                pltpu.SemaphoreType.DMA((2,)),
-                pltpu.SemaphoreType.DMA,
-                pltpu.SemaphoreType.DMA,
+                pltpu.SemaphoreType.DMA,
+                pltpu.SemaphoreType.DMA,
+                pltpu.SemaphoreType.DMA,
+                pltpu.SemaphoreType.DMA,
+                pltpu.SemaphoreType.DMA((heads,)),
                 pltpu.SemaphoreType.DMA((heads,)),
                 pltpu.SemaphoreType.DMA((heads,)),
                 pltpu.SemaphoreType.DMA((heads,)),

time: 109 us -> 103 us (0.945)
  the two profiles are of different devices: /device:TPU:49 before, /device:TPU:25 now
where the time goes in v4:
time: 103 us; the launch traced here: 102 us
  Pallas kernels  99.8 us (97%)
  local copies, waits for them, and re-layouts  2.69 us (3%)
    pallas_call x1, Pallas kernels, shards(): pl.pallas_call(functools.partial(kernel, n_ctx, n_head), out_shape=jax.Sh...  99.8 us
    unnamed x1, local copies, waits for them, and re-layouts  2.69 us

profile of v4, /device:TPU:25, one launch (start us, length us, event | category | flops | bytes accessed | tf_op | source)
XLA Modules:
  0.0 102.5 jit_solution(6344667633678388700)
XLA Ops:
  0.0 99.8 %shard_map.46 = bf16[128,6144]{1,0:T(8,128)(2,1)} custom-call(s32[6,8,18]{2,1,0:T(8,128)} %tiles_ref.1, bf16[128,6144]{1,0:T(8,128)(2,1)} %q_ref.1, bf16[128,6144]{1,0:T(8,128)(2,1)} %k_ref.1, bf16[128,6144]{1,0:T(8,128)(2,1)} %v_ref.1), custom_call_target="tpu_custom_call" | custom-call | tf_op jit(solution)/shard_map/pallas_call | solution.py:240
  99.8 2.7 %copy.6 = bf16[128,6144]{1,0:T(8,128)(2,1)} copy(bf16[128,6144]{1,0:T(8,128)(2,1)} %shard_map.46) | data formatting | bytes 3145728

commit v5 on v4

--- a/solution.py
+++ b/solution.py
@@ -178,13 +178,14 @@
             ).start()
 
     pass_halo(0)
+    pass_halo(1)
     relay(0)
 
     @pl.loop(0, heads)
     def _(j):
-        @pl.when(j + 1 < heads)
-        def _():
-            pass_halo(j + 1)
+        @pl.when(j + 2 < heads)
+        def _():
+            pass_halo(j + 2)
 
         pl.when(c != 0)(lambda: landed(j, 0, recv_below))
         pl.when(c != last)(lambda: landed(j, above, recv_above))
@@ -203,7 +204,7 @@
             for k in range(2):
                 gather(work, sc.at[k], ob, *lists[k], tops[k], j, tiles[k])
 
-            @pl.when((i == 4) & (j + 1 < heads))
+            @pl.when((i == 0) & (j + 1 < heads))
             def _():
                 relay(j + 1)
 

time: 103 us -> 100 us (0.971)
  the two profiles are of different devices: /device:TPU:25 before, /device:TPU:6 now
where the time goes in v5:
time: 100 us; the launch traced here: 98.6 us
  Pallas kernels  95.9 us (96%)
  local copies, waits for them, and re-layouts  2.69 us (3%)
    pallas_call x1, Pallas kernels, shards(): pl.pallas_call(functools.partial(kernel, n_ctx, n_head), out_shape=jax.Sh...  95.9 us
    unnamed x1, local copies, waits for them, and re-layouts  2.69 us

profile of v5, /device:TPU:6, one launch (start us, length us, event | category | flops | bytes accessed | tf_op | source)
XLA Modules:
  0.0 98.6 jit_solution(4497452263788897084)
XLA Ops:
  0.0 95.9 %shard_map.46 = bf16[128,6144]{1,0:T(8,128)(2,1)} custom-call(s32[6,8,18]{2,1,0:T(8,128)} %tiles_ref.1, bf16[128,6144]{1,0:T(8,128)(2,1)} %q_ref.1, bf16[128,6144]{1,0:T(8,128)(2,1)} %k_ref.1, bf16[128,6144]{1,0:T(8,128)(2,1)} %v_ref.1), custom_call_target="tpu_custom_call" | custom-call | tf_op jit(solution)/shard_map/pallas_call | solution.py:241
  95.9 2.7 %copy.6 = bf16[128,6144]{1,0:T(8,128)(2,1)} copy(bf16[128,6144]{1,0:T(8,128)(2,1)} %shard_map.46) | data formatting | bytes 3145728

commit v6 on v5

--- a/solution.py
+++ b/solution.py
@@ -53,8 +53,10 @@
     ob[j, t] = (numerator / row_total).astype(jnp.bfloat16)
 
 
-def kernel(n_ctx, n_head, tiles_ref, q_ref, k_ref, v_ref, out_ref, qb, kvb, passing, ob, work, sc, send_in, send_across_sem, send_halo, send_passing, send_out, recv_kv, recv_q, recv_below, recv_above, recv_passing, recv_out):
+def kernel(n_ctx, n_head, listed_ref, q_ref, k_ref, v_ref, out_ref, tiles_ref, qb, kvb, passing, ob, work, sc, send_in, send_across_sem, send_halo, send_passing, send_out, recv_kv, recv_q, recv_below, recv_above, recv_passing, recv_out, recv_tiles):
     heads = tiles_ref.shape[0]
+    lists = pltpu.make_async_copy(listed_ref, tiles_ref, recv_tiles)
+    lists.start()
     c, me = lax.axis_index("ctx"), lax.axis_index("head")
     base = (c - 1) * n_head
     turn, last = n_ctx // 2, n_ctx - 1
@@ -119,12 +121,13 @@
         send_tile(q_ref, lambda: qb.at[j, me], j, 2, recv_q.at[j])
 
     send_kv(0)
+    send_kv(1)
 
     @pl.loop(0, heads)
     def _(j):
-        @pl.when(j + 1 < heads)
-        def _():
-            send_kv(j + 1)
+        @pl.when(j + 2 < heads)
+        def _():
+            send_kv(j + 2)
 
         send_q(j)
 
@@ -177,6 +180,7 @@
                 recv_sem=recv_out, device_id=(c, t), device_id_type=MESH,
             ).start()
 
+    lists.wait()
     pass_halo(0)
     pass_halo(1)
     relay(0)
@@ -199,10 +203,10 @@
         @pl.loop(0, n_head, step=2)
         def _(i):
             tiles = [lax.rem(me + 1 + i + k, n_head) for k in range(2)]
-            lists = [listed_tiles(tiles_ref, j, t, base, n_head) for t in tiles]
-            tops = [score(qb, work, sc.at[k], lists[k][0], j, tiles[k]) for k in range(2)]
+            listed = [listed_tiles(tiles_ref, j, t, base, n_head) for t in tiles]
+            tops = [score(qb, work, sc.at[k], listed[k][0], j, tiles[k]) for k in range(2)]
             for k in range(2):
-                gather(work, sc.at[k], ob, *lists[k], tops[k], j, tiles[k])
+                gather(work, sc.at[k], ob, *listed[k], tops[k], j, tiles[k])
 
             @pl.when((i == 0) & (j + 1 < heads))
             def _():
@@ -241,9 +245,10 @@
         return pl.pallas_call(
             functools.partial(kernel, n_ctx, n_head),
             out_shape=jax.ShapeDtypeStruct(queries.shape, queries.dtype),
-            in_specs=[pl.BlockSpec(memory_space=pltpu.SMEM)] + [pl.BlockSpec(memory_space=pltpu.HBM)] * 3,
+            in_specs=[pl.BlockSpec(memory_space=pltpu.HBM)] * 4,
             out_specs=pl.BlockSpec(memory_space=pltpu.HBM),
             scratch_shapes=[
+                pltpu.SMEM(key_tiles.shape, jnp.int32),
                 pltpu.VMEM((heads, n_head, TILE, HDIM), jnp.bfloat16),
                 pltpu.VMEM((heads, 2, 3 * n_head, TILE, HDIM), jnp.bfloat16),
                 pltpu.VMEM((heads, n_head // 2, TILE, HDIM), jnp.bfloat16),
@@ -261,6 +266,7 @@
                 pltpu.SemaphoreType.DMA((heads,)),
                 pltpu.SemaphoreType.DMA((heads,)),
                 pltpu.SemaphoreType.DMA,
+                pltpu.SemaphoreType.DMA,
             ],
             compiler_params=pltpu.CompilerParams(
                 collective_id=0, has_side_effects=True, vmem_limit_bytes=67043328

time: 100 us -> 98.8 us (0.988)
  Pallas kernels: 95.9 us -> 94.2 us
    pallas_call x1, Pallas kernels: 95.9 us -> 94.2 us  [shards(): pl.pallas_call(functools.partial(kernel, n_ctx, n_head), out_shape=jax.Sh...]
where the time goes in v6:
time: 98.8 us; the launch traced here: 96.9 us
  Pallas kernels  94.2 us (95%)
  local copies, waits for them, and re-layouts  2.69 us (3%)
    pallas_call x1, Pallas kernels, shards(): pl.pallas_call(functools.partial(kernel, n_ctx, n_head), out_shape=jax.Sh...  94.2 us
    unnamed x1, local copies, waits for them, and re-layouts  2.69 us

profile of v6, /device:TPU:6, one launch (start us, length us, event | category | flops | bytes accessed | tf_op | source)
XLA Modules:
  0.0 96.9 jit_solution(17451586284458376365)
XLA Ops:
  0.0 94.2 %shard_map.46 = bf16[128,6144]{1,0:T(8,128)(2,1)} custom-call(s32[6,8,18]{2,1,0:T(8,128)} %listed_ref.1, bf16[128,6144]{1,0:T(8,128)(2,1)} %q_ref.1, bf16[128,6144]{1,0:T(8,128)(2,1)} %k_ref.1, bf16[128,6144]{1,0:T(8,128)(2,1)} %v_ref.1), custom_call_target="tpu_custom_call" | custom-call | tf_op jit(solution)/shard_map/pallas_call | solution.py:245
  94.2 2.7 %copy.6 = bf16[128,6144]{1,0:T(8,128)(2,1)} copy(bf16[128,6144]{1,0:T(8,128)(2,1)} %shard_map.46) | data formatting | bytes 3145728

commit v7 on v6

--- a/solution.py
+++ b/solution.py
@@ -25,24 +25,26 @@
     return ids, bias
 
 
-def score(qb, work, sc, ids, j, t):
+def score(qb, work, sc, ids, bias, j, t):
     query = qb[j, t]
     top = None
     for s in range(0, len(ids), 2):
         keys = jnp.concatenate([work[0, ids[s]], work[0, ids[s + 1]]], axis=0)
         scores = lax.dot_general(query, keys, (((1,), (1,)), ((), ())), preferred_element_type=jnp.float32)
-        sc[s] = scores[:, :TILE]
-        sc[s + 1] = scores[:, TILE:]
-        pair = jnp.maximum(scores[:, :TILE], scores[:, TILE:])
+        scores = scores * EXP2_SCALE
+        first, second = scores[:, :TILE] + bias[s], scores[:, TILE:] + bias[s + 1]
+        sc[s] = first
+        sc[s + 1] = second
+        pair = jnp.maximum(first, second)
         top = pair if top is None else jnp.maximum(top, pair)
     return jnp.max(top, axis=1, keepdims=True)
 
 
-def gather(work, sc, ob, ids, bias, row_max, j, t):
+def gather(work, sc, ob, ids, row_max, j, t):
     total, numerator = None, None
     for s in range(0, len(ids), 2):
-        first = jnp.exp2((sc[s] - row_max) * EXP2_SCALE + bias[s])
-        second = jnp.exp2((sc[s + 1] - row_max) * EXP2_SCALE + bias[s + 1])
+        first = jnp.exp2(sc[s] - row_max)
+        second = jnp.exp2(sc[s + 1] - row_max)
         pair = first + second
         total = pair if total is None else total + pair
         probs = jnp.concatenate([first.astype(jnp.bfloat16), second.astype(jnp.bfloat16)], axis=1)
@@ -95,7 +97,7 @@
     pl.semaphore_wait(barrier, greeted)
 
     def send_tile(source, place, j, sem_index, recv):
-        for p in range(1, n_head):
+        for p in (4, 3, 5, 2, 6, 1, 7):
             peer = lax.rem(me + p, n_head)
             pltpu.make_async_remote_copy(
                 src_ref=source.at[:, columns(peer, j)], dst_ref=place(), send_sem=send_in.at[sem_index],
@@ -112,10 +114,10 @@
             ).start()
 
     def send_kv(j):
+        pl.when(c == turn - 1)(lambda: send_across(j, turn, 0, recv_below))
+        pl.when(c == turn)(lambda: send_across(j, turn - 1, above, recv_above))
         send_tile(k_ref, lambda: kvb.at[j, 0, n_head + me], j, 0, recv_kv.at[j])
         send_tile(v_ref, lambda: kvb.at[j, 1, n_head + me], j, 1, recv_kv.at[j])
-        pl.when(c == turn - 1)(lambda: send_across(j, turn, 0, recv_below))
-        pl.when(c == turn)(lambda: send_across(j, turn - 1, above, recv_above))
 
     def send_q(j):
         send_tile(q_ref, lambda: qb.at[j, me], j, 2, recv_q.at[j])
@@ -204,9 +206,9 @@
         def _(i):
             tiles = [lax.rem(me + 1 + i + k, n_head) for k in range(2)]
             listed = [listed_tiles(tiles_ref, j, t, base, n_head) for t in tiles]
-            tops = [score(qb, work, sc.at[k], listed[k][0], j, tiles[k]) for k in range(2)]
+            tops = [score(qb, work, sc.at[k], *listed[k], j, tiles[k]) for k in range(2)]
             for k in range(2):
-                gather(work, sc.at[k], ob, *listed[k], tops[k], j, tiles[k])
+                gather(work, sc.at[k], ob, listed[k][0], tops[k], j, tiles[k])
 
             @pl.when((i == 0) & (j + 1 < heads))
             def _():

time: 98.8 us -> 98.3 us (level)
  no operation moved by 1% of the time
where the time goes in v7:
time: 98.3 us; the launch traced here: 97 us
  Pallas kernels  94.3 us (96%)
  local copies, waits for them, and re-layouts  2.69 us (3%)
    pallas_call x1, Pallas kernels, shards(): pl.pallas_call(functools.partial(kernel, n_ctx, n_head), out_shape=jax.Sh...  94.3 us
    unnamed x1, local copies, waits for them, and re-layouts  2.69 us

profile of v7, /device:TPU:6, one launch (start us, length us, event | category | flops | bytes accessed | tf_op | source)
XLA Modules:
  0.0 97.0 jit_solution(15783358352466619760)
XLA Ops:
  0.0 94.3 %shard_map.46 = bf16[128,6144]{1,0:T(8,128)(2,1)} custom-call(s32[6,8,18]{2,1,0:T(8,128)} %listed_ref.1, bf16[128,6144]{1,0:T(8,128)(2,1)} %q_ref.1, bf16[128,6144]{1,0:T(8,128)(2,1)} %k_ref.1, bf16[128,6144]{1,0:T(8,128)(2,1)} %v_ref.1), custom_call_target="tpu_custom_call" | custom-call | tf_op jit(solution)/shard_map/pallas_call | solution.py:247
  94.3 2.7 %copy.6 = bf16[128,6144]{1,0:T(8,128)(2,1)} copy(bf16[128,6144]{1,0:T(8,128)(2,1)} %shard_map.46) | data formatting | bytes 3145728
